TPU v7x, 128 devices: a whole 4x4x4 slice. The times are simulated.
128 devices in a mesh: dp: 8 (over z_hi, y), tensor: 16 (over x, z_lo, core).
Axes of the slice: x: 4, y: 4, z: 4 (z_hi: 2, z_lo: 2; z = z_hi * 2 + z_lo), core: 2. Of those that a mesh axis runs over, the one named last changes fastest.
Arguments:
- noisy: bfloat16 [64, 256, 1152], P('dp', None, 'tensor'), may hold values from -6 to 6
- labels: int32 [64], P('dp'), may hold values from 0 to 999
- tsteps: int32 [64], P('dp'), may hold values from 0 to 999
- guide_index: int32 [64], P('dp'), may hold values from 0 to 31
- class_table: bfloat16 [1001, 1152], replicated, may hold values from -6 to 6
- time_table: bfloat16 [1000, 1152], replicated, may hold values from -6 to 6
- guide_table: bfloat16 [32, 1152], replicated, may hold values from -6 to 6
- guide_weights: float32 [32], replicated, may hold values from 0.5 to 4
- teacher_qkv: bfloat16 [1152, 3456], P(None, 'tensor'), may hold values from -0.1875 to 0.1875
- teacher_out: bfloat16 [1152, 1152], P('tensor'), may hold values from -0.1875 to 0.1875
- teacher_ada: bfloat16 [3, 1152, 1152], P(None, None, 'tensor'), may hold values from -0.1875 to 0.1875
- student_qkv: bfloat16 [1152, 3456], P(None, 'tensor'), may hold values from -0.1875 to 0.1875
- student_out: bfloat16 [1152, 1152], P('tensor'), may hold values from -0.1875 to 0.1875
- student_ada: bfloat16 [3, 1152, 1152], P(None, None, 'tensor'), may hold values from -0.1875 to 0.1875
Outputs:
- grad_qkv: float32 [1152, 3456], P('dp', 'tensor')
- grad_out: float32 [1152, 1152], P('tensor', 'dp')
- grad_ada: float32 [3, 1152, 1152], P(None, 'dp', 'tensor')
All inputs are finite; a program needn't handle non-finite values.
Results may differ from a plain program's by a relative error of at most 0.034.
Values may be sent and summed in bfloat16 or wider, within the bound.
A program may use at most 128 MiB of HBM per device.

v0:
```python
import math
import jax
import jax.numpy as jnp
from jax import lax
from jax.sharding import PartitionSpec as P

HD = 72
norm_eps = 1e-06


def in_order(pieces, dim):
    shape = list(pieces.shape[1:])
    shape[dim] *= pieces.shape[0]
    return jnp.moveaxis(pieces, 0, dim).reshape(shape)


def sent_to_all(shard, axis):
    copies = jnp.broadcast_to(shard, (lax.axis_size(axis), *shard.shape))
    return lax.all_to_all(copies, axis, split_axis=0, concat_axis=0, tiled=True)


def collect(shard, axis, dim):
    return in_order(sent_to_all(shard, axis), dim)


def taken_together(shard, axis):
    return sent_to_all(shard, axis).sum(axis=0)


def in_one(arrays, axis):
    vector, at, outs = (jnp.concatenate([a.reshape(-1) for a in arrays]), 0, [])
    running = taken_together(vector, axis)
    for a in arrays:
        outs.append(running[at : at + a.size].reshape(a.shape))
        at += a.size
    return tuple(outs)


def in_blocks(shard, dim, devices):
    shape = shard.shape
    pieces = shard.reshape(*shape[:dim], devices, shape[dim] // devices, *shape[dim + 1 :])
    return jnp.moveaxis(pieces, dim, 0)


def sum_together(arrays, axis, dims):
    devices = lax.axis_size(axis)
    pieces = [in_blocks(a, dim, devices) for a, dim in zip(arrays, dims)]
    lines = jnp.concatenate([b.reshape(devices, -1) for b in pieces], axis=1)
    span = max(16, -(-lines.shape[1] // 1024) * 8)
    lines = jnp.pad(lines, ((0, 0), (0, span * 128 - lines.shape[1]))).reshape(-1, 128)
    vector, at, outs = (lax.psum_scatter(lines, axis, tiled=True).reshape(-1), 0, [])
    for b in pieces:
        part = b[0]
        outs.append(vector[at : at + part.size].reshape(part.shape))
        at += part.size
    return tuple(outs)


def lookup_rows(indices, table_rows):
    one_hot = (
        indices[:, None] == jnp.arange(table_rows.shape[0], dtype=jnp.int32)[None, :]
    ).astype(table_rows.dtype)
    return jnp.dot(one_hot, table_rows, preferred_element_type=jnp.float32)


def attend(qkv_sums, heads_here):
    batch_rows, seq_len = (qkv_sums.shape[0], qkv_sums.shape[1])
    heads_qkv = qkv_sums.astype(jnp.bfloat16).reshape(batch_rows, seq_len, heads_here, 3, HD)
    queries, key_rows, values = (
        heads_qkv[:, :, :, 0],
        heads_qkv[:, :, :, 1],
        heads_qkv[:, :, :, 2],
    )
    scores = jnp.einsum(
        "blhe,bmhe->bhlm", queries, key_rows, preferred_element_type=jnp.float32
    ) * (1.0 / math.sqrt(HD))
    exponent = jnp.exp(scores - jnp.max(scores, axis=-1, keepdims=True))
    attn_prob = exponent / jnp.sum(exponent, axis=-1, keepdims=True)
    prob_low = attn_prob.astype(jnp.bfloat16)
    attn_mixed = jnp.einsum("bhlm,bmhe->blhe", prob_low, values, preferred_element_type=jnp.float32)
    attn_mixed = attn_mixed.astype(jnp.bfloat16).reshape(batch_rows, seq_len, heads_here * HD)
    return (heads_qkv, attn_prob, prob_low, attn_mixed)


def attend_grad(heads_qkv, attn_prob, prob_low, grad_low):
    batch_rows, seq_len = (heads_qkv.shape[0], heads_qkv.shape[1])
    queries, key_rows, values = (
        heads_qkv[:, :, :, 0],
        heads_qkv[:, :, :, 1],
        heads_qkv[:, :, :, 2],
    )
    grad_probs = jnp.einsum("blhe,bmhe->bhlm", grad_low, values, preferred_element_type=jnp.float32)
    row_delta = jnp.sum(attn_prob * grad_probs, axis=-1, keepdims=True)
    grad_scores = (attn_prob * (grad_probs - row_delta) * (1.0 / math.sqrt(HD))).astype(
        jnp.bfloat16
    )
    grad_query = jnp.einsum(
        "bhlm,bmhe->blhe", grad_scores, key_rows, preferred_element_type=jnp.float32
    )
    grad_keys = jnp.einsum(
        "bhlm,blhe->bmhe", grad_scores, queries, preferred_element_type=jnp.float32
    )
    grad_values = jnp.einsum(
        "bhlm,blhe->bmhe", prob_low, grad_low, preferred_element_type=jnp.float32
    )
    grad_qkv_act = jnp.stack([grad_query, grad_keys, grad_values], axis=3).astype(jnp.bfloat16)
    return grad_qkv_act.reshape(batch_rows, seq_len, -1)


def forward(normed, wide_mod, qkv_weight, heads_here):
    full_rows = (
        normed.astype(jnp.float32) * (1.0 + wide_mod[:, 1][:, None]) + wide_mod[:, 0][:, None]
    ).astype(jnp.bfloat16)
    qkv_sums = jnp.einsum("bld,df->blf", full_rows, qkv_weight, preferred_element_type=jnp.float32)
    return attend(qkv_sums, heads_here)


def local(
    noisy,
    labels,
    tsteps,
    guide_index,
    class_table,
    time_table,
    guide_table,
    guide_weights,
    teacher_qkv,
    teacher_out,
    teacher_ada,
    student_qkv,
    student_out,
    student_ada,
):
    samples, seq_len, width_part = noisy.shape
    model_width = width_part * lax.axis_size("tensor")
    dp = lax.axis_size("dp")
    batch_size = samples * dp
    heads_here = student_out.shape[0] // HD
    wide = lax.all_gather(noisy, "tensor", axis=2, tiled=True)
    null_class = class_table.shape[0] - 1
    time_embed = lookup_rows(tsteps, time_table)
    cond_embed = lookup_rows(labels, class_table) + time_embed
    null_embed = class_table[null_class].astype(jnp.float32)[None, :] + time_embed
    guide_hot = guide_index[:, None] == jnp.arange(guide_table.shape[0], dtype=jnp.int32)[None, :]
    student_embed = cond_embed + jnp.dot(
        guide_hot.astype(jnp.bfloat16), guide_table, preferred_element_type=jnp.float32
    )
    strength = jnp.sum(jnp.where(guide_hot, guide_weights[None, :], 0.0), axis=1)
    cond_act = jax.nn.silu(cond_embed).astype(jnp.bfloat16)
    null_act = jax.nn.silu(null_embed).astype(jnp.bfloat16)
    student_act = jax.nn.silu(student_embed).astype(jnp.bfloat16)
    teacher_act = jnp.concatenate([cond_act, null_act], axis=0)
    mod_t = jnp.einsum("bd,kde->bke", teacher_act, teacher_ada, preferred_element_type=jnp.float32)
    mod_s = jnp.einsum("bd,kde->bke", student_act, student_ada, preferred_element_type=jnp.float32)
    wide_mod = collect(jnp.concatenate([mod_t, mod_s], axis=0), "tensor", 2)
    cond_mod, null_mod, student_mod = (
        wide_mod[:samples],
        wide_mod[samples : 2 * samples],
        wide_mod[2 * samples :],
    )
    scale_norm = 1.0 / math.sqrt(batch_size * seq_len)
    signal = wide.astype(jnp.float32)
    row_mean = jnp.sum(signal, axis=2) / model_width
    row_var = jnp.sum(signal * signal, axis=2) / model_width - row_mean * row_mean
    normed = ((signal - row_mean[:, :, None]) * lax.rsqrt(row_var + norm_eps)[:, :, None]).astype(
        jnp.bfloat16
    )
    teacher_mixed = forward(
        jnp.concatenate([normed, normed], axis=0), wide_mod[: 2 * samples], teacher_qkv, heads_here
    )[3]
    heads_qkv, attn_prob, prob_low, attn_mixed = forward(
        normed, student_mod, student_qkv, heads_here
    )
    teacher_part = jnp.einsum(
        "blf,fd->bld", teacher_mixed, teacher_out, preferred_element_type=jnp.float32
    )
    student_part = jnp.einsum(
        "blf,fd->bld", attn_mixed, student_out, preferred_element_type=jnp.float32
    )
    gate = student_mod[:, 2] * scale_norm
    cond_gate = (1.0 + strength)[:, None] * cond_mod[:, 2] * scale_norm
    null_gate = strength[:, None] * null_mod[:, 2] * scale_norm
    partial_cot = (
        gate[:, None] * student_part
        - cond_gate[:, None] * teacher_part[:samples]
        + null_gate[:, None] * teacher_part[samples:]
    )
    piece = lax.psum_scatter(
        partial_cot.astype(jnp.bfloat16), "tensor", scatter_dimension=2, tiled=True
    )
    cotangent = lax.all_gather(piece, "tensor", axis=2, tiled=True)
    grad_proj = (cotangent.astype(jnp.float32) * student_mod[:, 2][:, None]).astype(jnp.bfloat16)
    grad_mixed = jnp.einsum(
        "bld,ed->ble", grad_proj, student_out, preferred_element_type=jnp.float32
    )
    image_out = jnp.einsum(
        "ble,bld->bed", attn_mixed, cotangent, preferred_element_type=jnp.float32
    )
    grad_out_rows = jnp.sum(image_out * student_mod[:, 2][:, None], axis=0)
    grad_gate = jnp.sum(image_out * student_out.astype(jnp.float32)[None], axis=1)
    grad_low = grad_mixed.astype(jnp.bfloat16).reshape(samples, seq_len, heads_here, HD)
    grad_qkv_act = attend_grad(heads_qkv, attn_prob, prob_low, grad_low)
    image_qkv = jnp.einsum("bld,blf->bdf", normed, grad_qkv_act, preferred_element_type=jnp.float32)
    column_sums = jnp.sum(grad_qkv_act.astype(jnp.float32), axis=1)
    grad_qkv_local = jnp.sum(
        image_qkv * (1.0 + student_mod[:, 1])[:, :, None]
        + student_mod[:, 0][:, :, None] * column_sums[:, None, :],
        axis=0,
    )
    weight = student_qkv.astype(jnp.float32)
    grad_scale = jnp.sum(image_qkv * weight[None], axis=2)
    grad_shift = jnp.einsum("bf,df->bd", column_sums, weight, precision=lax.Precision.HIGHEST)
    grad_modulation = lax.psum_scatter(
        jnp.stack([grad_shift, grad_scale, grad_gate], axis=1),
        "tensor",
        scatter_dimension=2,
        tiled=True,
    )
    all_mod = lax.all_gather(grad_modulation, "dp", axis=0, tiled=True)
    act_rows = lax.all_to_all(student_act, "dp", split_axis=1, concat_axis=0, tiled=True)
    grad_ada = jnp.einsum(
        "bd,bke->kde", act_rows.astype(jnp.float32), all_mod, precision=lax.Precision.HIGHEST
    )
    grad_qkv = lax.psum_scatter(
        grad_qkv_local.astype(jnp.bfloat16), "dp", scatter_dimension=0, tiled=True
    ).astype(jnp.float32)
    grad_out = lax.psum_scatter(
        grad_out_rows.astype(jnp.bfloat16), "dp", scatter_dimension=1, tiled=True
    ).astype(jnp.float32)
    return (grad_qkv, grad_out, grad_ada)


def solution(mesh):
    return jax.shard_map(
        local,
        mesh=mesh,
        in_specs=(
            P("dp", None, "tensor"),
            P("dp"),
            P("dp"),
            P("dp"),
            P(),
            P(),
            P(),
            P(),
            P(None, "tensor"),
            P("tensor", None),
            P(None, None, "tensor"),
            P(None, "tensor"),
            P("tensor", None),
            P(None, None, "tensor"),
        ),
        out_specs=(P("dp", "tensor"), P("tensor", "dp"), P(None, "dp", "tensor")),
        check_vma=False,
    )
```

profile of v0, /device:TPU:0, one launch (start us, length us, event | category | flops | bytes accessed | tf_op | source)
XLA Modules:
  0.0 511.6 jit_solution(7823777829901788523)
XLA Ops:
  7.3 0.7 all-gather.3.cloned.1.call-update
  8.0 1.0 convert_reduce_fusion.2
  9.0 1.1 multiply_convert_fusion.6
  10.1 2.2 multiply_convert_fusion.7
  13.1 0.9 broadcast_in_dim.10
  14.0 5.9 %all-to-all-start = ((f32[16,24,3,72]{3,1,2,0:T(8,128)}), f32[16,24,3,72]{3,1,2,0:T(8,128)S(1)}, u32[]{:S(2)}, u32[]{:S(2)}) async-start(f32[16,24,3,72]{3,1,2,0:T(8,128)} %broadcast_in_dim.10), calls=%async_computation | async-start | bytes 1179648 | tf_op jit(solution)/shard_map/all_to_all | solution.py:19
  20.1 14.4 %all-to-all-done = f32[16,24,3,72]{3,1,2,0:T(8,128)S(1)} async-done(((f32[16,24,3,72]{3,1,2,0:T(8,128)}), f32[16,24,3,72]{3,1,2,0:T(8,128)S(1)}, u32[]{:S(2)}, u32[]{:S(2)}) %all-to-all-start) | async-done | bytes 331808 | tf_op jit(solution)/shard_map/all_to_all | solution.py:19
  35.6 20.1 %all-gather.3.cloned.1.call-done = bf16[8,256,1152]{1,2,0:T(8,128)(2,1)} async-done(((bf16[8,256,72]{1,2,0:T(8,128)(2,1)}), bf16[8,256,1152]{1,2,0:T(8,128)(2,1)}) %all-gather.3.cloned.1.call-update) | async-done | bytes 4718608 | tf_op jit(solution)/shard_map/all_gather | solution.py:139
  55.7 3.7 convert_reduce_fusion
  59.5 1.1 fusion.4
  60.6 9.5 %fusion.29 = bf16[16,256,216]{1,2,0:T(8,128)(2,1)S(1)} fusion(bf16[8,256,1152]{1,2,0:T(8,128)(2,1)S(1)} %fusion.4, f32[16,1152]{1,0:T(8,128)S(1)} %get-tuple-element.33, f32[16,1152]{1,0:T(8,128)S(1)} %get-tuple-element.32, bf16[1152,216]{0,1:T(8,128)(2,1)S(1)} %copy-done.11), kind=kOutput, calls=%fused_computation.49 | convolution fusion | flops 2062909440 | bytes 7133184 | tf_op jit(solution)/shard_map/bld,df->blf/dot_general | solution.py:114
  70.1 0.8 fusion.51
  70.9 1.1 fusion.97
  72.3 5.4 %fusion.36 = bf16[8,256,216]{1,2,0:T(8,128)(2,1)} fusion(bf16[8,256,1152]{1,2,0:T(8,128)(2,1)S(1)} %fusion.4, f32[8,1152]{1,0:T(8,128)S(1)} %get-tuple-element.36, f32[8,1152]{1,0:T(8,128)S(1)} %get-tuple-element.37, bf16[1152,216]{0,1:T(8,128)(2,1)S(1)} %copy-done.5), kind=kOutput, calls=%fused_computation.52 | convolution fusion | flops 1029095424 | bytes 6174720 | tf_op jit(solution)/shard_map/bld,df->blf/dot_general | solution.py:114
  77.7 3.3 fusion.98
  81.0 11.7 %fusion.39 = f32[16,256,1152]{1,2,0:T(8,128)} fusion(f32[16,256]{1,0:T(8,128)S(1)} %fusion.97, bf16[16,256,1,3,72]{1,4,3,0,2:T(8,128)(2,1)S(1)} %bitcast.190, f32[16,256,256]{1,2,0:T(8,128)} %copy-done.4, bf16[72,1152]{1,0:T(8,128)(2,1)S(1)} %copy-done.8), kind=kOutput, calls=%fused_computation.55 | convolution fusion | flops 836014336 | bytes 28035072 | tf_op jit(solution)/shard_map/blf,fd->bld/dot_general | solution.py:174
  92.7 2.1 fusion.47
  94.7 11.0 %fusion.99 = bf16[144,8,8,256]{3,1,0,2:T(8,128)(2,1)S(1)} fusion(f32[16,256,1152]{1,2,0:T(8,128)} %fusion.39, f32[8,1152]{1,0:T(8,128)S(1)} %fusion.69, f32[8,1152]{1,0:T(8,128)S(1)} %get-tuple-element.46, bf16[8,256,72]{1,2,0:T(8,128)(2,1)S(1)} %fusion.47, bf16[72,1152]{1,0:T(8,128)(2,1)S(1)} %copy-done.9, f32[8,1152]{1,0:T(8,128)S(1)} %get-tuple-element.35), kind=kOutput, calls=%fused_computation.135 | convolution fusion | flops 353894400 | bytes 24164352 | tf_op jit(solution)/shard_map/blf,fd->bld/dot_general | solution.py:177
  105.8 2.8 copy.180
  108.8 69.7 %reduce-scatter.11.cloned.1.call-done = bf16[72,2048]{1,0:T(8,128)(2,1)} async-done(((bf16[1152,2048]{1,0:T(8,128)(2,1)}), bf16[72,2048]{1,0:T(8,128)(2,1)}) %reduce-scatter.11.cloned.1.call-update) | async-done | bytes 294928
  178.5 1.0 copy.181
  179.6 0.8 copy.167
  180.4 1.0 convert_element_type.156
  181.5 35.3 %all-gather.5.cloned.1.call-done = bf16[8,256,1152]{1,2,0:T(8,128)(2,1)} async-done(((bf16[8,256,72]{1,2,0:T(8,128)(2,1)}), bf16[8,256,1152]{1,2,0:T(8,128)(2,1)}) %all-gather.5.cloned.1.call-update) | async-done | bytes 4718608 | tf_op jit(solution)/shard_map/all_gather | solution.py:191
  216.8 4.3 fusion.46
  221.1 2.1 convolution_bitcast_fusion.1
  223.1 1.5 fusion.63
  224.6 3.8 fusion.43
  228.4 3.8 fusion.40
  232.2 1.5 convert_reduce_fusion.1
  234.2 6.2 %multiply_reduce_fusion = (f32[8,1152]{1,0:T(8,128)S(1)}, bf16[1152,216]{0,1:T(8,128)(2,1)S(1)}) fusion(f32[1152,216]{0,1:T(8,128)} %convert_element_type.156, f32[8,216]{1,0:T(8,128)S(1)} %mul.229, f32[8,1152]{1,0:T(8,128)S(1)} %get-tuple-element.36, f32[8,1152]{1,0:T(8,128)} %copy-done.10, bf16[8,256,1152]{1,2,0:T(8,128)(2,1)} %copy-done.3, ...), kind=kOutput, calls=%fused_computation.23 | convolution fusion | flops 1030901760 | bytes 7213824 | tf_op jit(solution)/shard_map/bld,blf->bdf/dot_general | solution.py:203
  240.5 1.6 multiply_reduce_fusion.2
  242.1 0.7 pad_maximum_fusion
  242.9 0.9 copy.170
  243.8 1.1 copy.168
  245.0 0.6 copy.153
  245.7 6.9 %all-to-all-start.1 = ((bf16[8,8,144]{2,0,1:T(8,128)(2,1)}), bf16[8,8,144]{2,0,1:T(8,128)(2,1)S(1)}, u32[]{:S(2)}, u32[]{:S(2)}) async-start(bf16[8,8,144]{2,0,1:T(8,128)(2,1)} %copy.153), calls=%async_computation.1 | async-start | bytes 65536 | tf_op jit(solution)/shard_map/all_to_all | solution.py:220
  252.5 0.6 dynamic-slice
  253.7 103.5 %all-reduce.3.cloned.1.call-done = f32[8,3,1152]{2,0,1:T(8,128)} async-done(((f32[8,3,1152]{2,0,1:T(8,128)}), f32[8,3,1152]{2,0,1:T(8,128)}) %all-reduce.3.cloned.1.call-update) | async-done | bytes 110608
  357.2 0.8 constant_dynamic-slice_fusion
  358.0 34.5 %all_gather.11 = f32[64,3,72]{2,0,1:T(8,128)S(1)} all-gather(f32[8,3,72]{2,0,1:T(8,128)S(1)} %constant_dynamic-slice_fusion), channel_id=1, replica_groups=mesh['dp'=8,'tensor'=16] {'dp'}, dimensions={0}, use_global_device_ids=true | all-gather | bytes 62208 | tf_op jit(solution)/shard_map/all_gather | solution.py:219
  392.8 0.8 copy.155
  393.6 34.5 %reduce-scatter.15.cloned.1.call-done = bf16[144,72]{1,0:T(8,128)(2,1)} async-done(((bf16[1152,72]{1,0:T(8,128)(2,1)}), bf16[144,72]{1,0:T(8,128)(2,1)}) %reduce-scatter.15.cloned.1.call-update) | async-done | bytes 20752
  428.1 0.8 copy.171
  429.0 0.6 convert_element_type.155
  429.6 73.3 %reduce-scatter.13.cloned.1.call-done = bf16[144,216]{1,0:T(8,128)(2,1)} async-done(((bf16[1152,216]{1,0:T(8,128)(2,1)}), bf16[144,216]{1,0:T(8,128)(2,1)}) %reduce-scatter.13.cloned.1.call-update) | async-done | bytes 62224
  503.0 1.0 copy.169
  503.9 0.8 copy.154
  (80 shorter events, 3.9 us)
Async XLA Ops:
  7.2 1.8 copy-start
  7.2 5.1 copy-start.12
  7.2 5.1 copy-start.13
  7.2 5.3 %copy-start.6 = (bf16[3,1152,72]{1,2,0:T(8,128)(2,1)S(1)}, bf16[3,1152,72]{1,2,0:T(8,128)(2,1)}, u32[]{:S(2)}) copy-start(bf16[3,1152,72]{1,2,0:T(8,128)(2,1)} %param.24) | copy-start | bytes 1492996
  7.2 5.6 %copy-start.7 = (bf16[3,1152,72]{1,2,0:T(8,128)(2,1)S(1)}, bf16[3,1152,72]{1,2,0:T(8,128)(2,1)}, u32[]{:S(2)}) copy-start(bf16[3,1152,72]{1,2,0:T(8,128)(2,1)} %param.27) | copy-start | bytes 1492996
  7.2 12.7 %copy-start.14 = (f32[32]{0:T(128)S(1)}, f32[32]{0:T(128)}, u32[]{:S(2)}) copy-start(f32[32]{0:T(128)} %param.21) | copy-start | bytes 388
  7.2 48.5 %all-gather.3.cloned.1.call-start = ((), (), s32[]{:S(2)}) async-start(), calls=%async_computation.5 | async-start | bytes 5013504 | tf_op jit(solution)/shard_map/all_gather | solution.py:139
  14.0 20.5 %all-to-all-start = ((f32[16,24,3,72]{3,1,2,0:T(8,128)}), f32[16,24,3,72]{3,1,2,0:T(8,128)S(1)}, u32[]{:S(2)}, u32[]{:S(2)}) async-start(f32[16,24,3,72]{3,1,2,0:T(8,128)} %broadcast_in_dim.10), calls=%async_computation | async-start | bytes 1179648 | tf_op jit(solution)/shard_map/all_to_all | solution.py:19
  19.9 158.7 %reduce-scatter.11.cloned.1.call-start = ((), (), s32[]{:S(2)}) async-start(), calls=%async_computation.7 | async-start | bytes 5013504
  35.6 36.4 %copy-start.10 = (f32[8,1152]{1,0:T(8,128)}, f32[8,1152]{1,0:T(8,128)S(1)}, u32[]{:S(2)}) copy-start(f32[8,1152]{1,0:T(8,128)S(1)} %get-tuple-element.37) | copy-start | bytes 110596
  55.7 3.8 copy-start.2
  59.5 1.2 copy-start.11
  60.6 11.4 %copy-start.3 = (bf16[8,256,1152]{1,2,0:T(8,128)(2,1)}, bf16[8,256,1152]{1,2,0:T(8,128)(2,1)S(1)}, u32[]{:S(2)}) copy-start(bf16[8,256,1152]{1,2,0:T(8,128)(2,1)S(1)} %fusion.4) | copy-start | bytes 14155780
  70.9 6.8 %copy-start.4 = (f32[16,256,256]{1,2,0:T(8,128)}, f32[16,256,256]{1,2,0:T(8,128)S(1)}, u32[]{:S(2)}) copy-start(f32[16,256,256]{1,2,0:T(8,128)S(1)} %fusion.51) | copy-start | bytes 12582916
  70.9 1.4 copy-start.5
  72.3 8.7 %copy-start.8 = (bf16[72,1152]{1,0:T(8,128)(2,1)S(1)}, bf16[72,1152]{1,0:T(8,128)(2,1)}, u32[]{:S(2)}) copy-start(bf16[72,1152]{1,0:T(8,128)(2,1)} %param.23) | copy-start | bytes 497668
  92.7 2.1 copy-start.9
  94.7 11.0 %copy-start.16 = (bf16[8,256,72]{1,2,0:T(8,128)(2,1)}, bf16[8,256,72]{1,2,0:T(8,128)(2,1)S(1)}, u32[]{:S(2)}) copy-start(bf16[8,256,72]{1,2,0:T(8,128)(2,1)S(1)} %fusion.47) | copy-start | bytes 884740
  108.6 108.2 %all-gather.5.cloned.1.call-start = ((), (), s32[]{:S(2)}) async-start(), calls=%async_computation.6 | async-start | bytes 5013504 | tf_op jit(solution)/shard_map/all_gather | solution.py:191
  180.4 176.9 %all-reduce.3.cloned.1.call-start = ((), (), s32[]{:S(2)}) async-start(), calls=%async_computation.10 | async-start | bytes 221184
  233.8 6.7 %slice-start = ((s8[4718592]{0:T(1024)(128)(4,1)}), s8[4194304]{0:T(1024)(128)(4,1)S(1)}, s32[]{:S(2)}) async-start(s8[4718592]{0:T(1024)(128)(4,1)} %bitcast.203), calls=%async_computation.11 | async-start | bytes 8388608
  234.2 6.3 %slice-start.1 = ((s8[4718592]{0:T(1024)(128)(4,1)}), s8[524288]{0:T(1024)(128)(4,1)S(1)}, s32[]{:S(2)}) async-start(s8[4718592]{0:T(1024)(128)(4,1)} %bitcast.203), calls=%async_computation.12 | async-start | bytes 1048576
  234.2 6.3 %copy-start.17 = (bf16[8,256,72]{1,2,0:T(8,128)(2,1)S(1)}, bf16[8,256,72]{1,2,0:T(8,128)(2,1)}, u32[]{:S(2)}) copy-start(bf16[8,256,72]{1,2,0:T(8,128)(2,1)} %copy-done.16) | copy-start | bytes 884740
  234.2 270.5 %copy-start.1 = (bf16[1000,1152]{1,0:T(8,128)(2,1)S(1)}, bf16[1000,1152]{1,0:T(8,128)(2,1)}, u32[]{:S(2)}) copy-start(bf16[1000,1152]{1,0:T(8,128)(2,1)} %param.19) | copy-start | bytes 6912004
  240.5 12.0 %copy-start.15 = (u32[128]{0:T(128)S(1)}, u32[128]{0:T(128)}, u32[]{:S(2)}) copy-start(u32[128]{0:T(128)} %constant.33) | copy-start | bytes 1540
  242.8 185.3 %reduce-scatter.15.cloned.1.call-start = ((), (), s32[]{:S(2)}) async-start(), calls=%async_computation.9 | async-start | bytes 331776
  243.8 259.2 %reduce-scatter.13.cloned.1.call-start = ((), (), s32[]{:S(2)}) async-start(), calls=%async_computation.8 | async-start | bytes 663552
  245.7 146.8 %all-to-all-start.1 = ((bf16[8,8,144]{2,0,1:T(8,128)(2,1)}), bf16[8,8,144]{2,0,1:T(8,128)(2,1)S(1)}, u32[]{:S(2)}, u32[]{:S(2)}) async-start(bf16[8,8,144]{2,0,1:T(8,128)(2,1)} %copy.153), calls=%async_computation.1 | async-start | bytes 65536 | tf_op jit(solution)/shard_map/all_to_all | solution.py:220
Sparse Core Ops, SparseCore 0:
  9.7 45.9 all-gather.2
  108.7 69.8 reduce-scatter.10
  180.5 36.2 all-gather.4
  242.9 114.2 all-reduce.2
  360.7 67.4 reduce-scatter.14
  431.6 71.3 reduce-scatter.12
where the time goes:
time: 512 us
  waiting for transfers between devices  352 us (69%)
  matrix products  71.6 us (14%)
  blocking collectives  34.5 us (7%)
  between operations  15.1 us (3%)
  local copies, waits for them, and re-layouts  14.4 us (3%)
  starting transfers between devices  13.1 us (3%)
  other arithmetic  11.2 us (2%)
    unnamed x10, waiting for transfers between devices  282 us
    all_gather x1, waiting for transfers between devices, local(): cotangent = lax.all_gather(piece, 'tensor', axis=2, tiled=True)  35.3 us
    all_gather x1, blocking collectives, local(): all_mod = lax.all_gather(grad_modulation, 'dp', axis=0, tiled=True)  34.5 us
    all_gather x1, waiting for transfers between devices, local(): wide = lax.all_gather(noisy, 'tensor', axis=2, tiled=True)  20.1 us
    dot_general x2, matrix products, forward(): jnp.einsum('bld,df->blf', full_rows, qkv_weight, preferred_element_type=j...  14.9 us
    all_to_all x1, waiting for transfers between devices, sent_to_all(): return lax.all_to_all(copies, axis, split_axis=0, concat_axis=0, tiled=True)  14.4 us
    unnamed x51, local copies, waits for them, and re-layouts  11.8 us
    dot_general x1, matrix products, local(): jnp.einsum('blf,fd->bld', teacher_mixed, teacher_out, preferred_element_t...  11.7 us
  transfers between devices with their start and end apart: 8, of which 7 were waited for; matrix products, arithmetic and copies ran while one was open for 3% of the time, Pallas kernels for 0%

commit v1 on v0

--- a/solution.py
+++ b/solution.py
@@ -188,7 +188,8 @@
     piece = lax.psum_scatter(
         partial_cot.astype(jnp.bfloat16), "tensor", scatter_dimension=2, tiled=True
     )
-    cotangent = lax.all_gather(piece, "tensor", axis=2, tiled=True)
+    y2 = lax.all_gather(piece, "tensor")
+    cotangent = jnp.concatenate(y2, 2)
     grad_proj = (cotangent.astype(jnp.float32) * student_mod[:, 2][:, None]).astype(jnp.bfloat16)
     grad_mixed = jnp.einsum(
         "bld,ed->ble", grad_proj, student_out, preferred_element_type=jnp.float32

time: 512 us -> 515 us (level)
    unnamed x51 -> x47, local copies, waits for them, and re-layouts: 11.8 us -> 12.6 us
where the time goes in v1:
time: 515 us; the launch traced here: 514 us
  waiting for transfers between devices  352 us (68%)
  matrix products  70.3 us (14%)
  blocking collectives  34.5 us (7%)
  local copies, waits for them, and re-layouts  17.9 us (3%)
  between operations  15.1 us (3%)
  starting transfers between devices  13.1 us (3%)
  other arithmetic  11.2 us (2%)
    unnamed x10, waiting for transfers between devices  282 us
    all_gather x1, waiting for transfers between devices, local(): y2 = lax.all_gather(piece, 'tensor')  35.4 us
    all_gather x1, blocking collectives, local(): all_mod = lax.all_gather(grad_modulation, 'dp', axis=0, tiled=True)  34.5 us
    all_gather x1, waiting for transfers between devices, local(): wide = lax.all_gather(noisy, 'tensor', axis=2, tiled=True)  20.1 us
    dot_general x2, matrix products, forward(): jnp.einsum('bld,df->blf', full_rows, qkv_weight, preferred_element_type=j...  14.9 us
    all_to_all x1, waiting for transfers between devices, sent_to_all(): return lax.all_to_all(copies, axis, split_axis=0, concat_axis=0, tiled=True)  14.4 us
    unnamed x47, local copies, waits for them, and re-layouts  12.6 us
    dot_general x1, matrix products, local(): jnp.einsum('blf,fd->bld', teacher_mixed, teacher_out, preferred_element_t...  11.7 us
  transfers between devices with their start and end apart: 8, of which 7 were waited for; matrix products, arithmetic and copies ran while one was open for 3% of the time, Pallas kernels for 0%

profile of v1, /device:TPU:0, one launch (start us, length us, event | category | flops | bytes accessed | tf_op | source)
XLA Modules:
  0.0 513.7 jit_solution(9893021585539589534)
XLA Ops:
  7.3 0.7 all-gather.4.cloned.1.call-update
  8.0 1.0 convert_reduce_fusion.2
  9.0 1.1 multiply_convert_fusion.6
  10.1 2.2 multiply_convert_fusion.7
  13.1 0.9 broadcast_in_dim.10
  14.0 5.9 %all-to-all-start = ((f32[16,24,3,72]{3,1,2,0:T(8,128)}), f32[16,24,3,72]{3,1,2,0:T(8,128)S(1)}, u32[]{:S(2)}, u32[]{:S(2)}) async-start(f32[16,24,3,72]{3,1,2,0:T(8,128)} %broadcast_in_dim.10), calls=%async_computation | async-start | bytes 1179648 | tf_op jit(solution)/shard_map/all_to_all | solution.py:19
  20.1 14.4 %all-to-all-done = f32[16,24,3,72]{3,1,2,0:T(8,128)S(1)} async-done(((f32[16,24,3,72]{3,1,2,0:T(8,128)}), f32[16,24,3,72]{3,1,2,0:T(8,128)S(1)}, u32[]{:S(2)}, u32[]{:S(2)}) %all-to-all-start) | async-done | bytes 331808 | tf_op jit(solution)/shard_map/all_to_all | solution.py:19
  35.6 20.1 %all-gather.4.cloned.1.call-done = bf16[8,256,1152]{1,2,0:T(8,128)(2,1)} async-done(((bf16[8,256,72]{1,2,0:T(8,128)(2,1)}), bf16[8,256,1152]{1,2,0:T(8,128)(2,1)}) %all-gather.4.cloned.1.call-update) | async-done | bytes 4718608 | tf_op jit(solution)/shard_map/all_gather | solution.py:139
  55.7 3.7 convert_reduce_fusion
  59.5 1.1 fusion.4
  60.6 9.5 %fusion.29 = bf16[16,256,216]{1,2,0:T(8,128)(2,1)S(1)} fusion(bf16[8,256,1152]{1,2,0:T(8,128)(2,1)S(1)} %fusion.4, f32[16,1152]{1,0:T(8,128)S(1)} %get-tuple-element.33, f32[16,1152]{1,0:T(8,128)S(1)} %get-tuple-element.32, bf16[1152,216]{0,1:T(8,128)(2,1)S(1)} %copy-done.11), kind=kOutput, calls=%fused_computation.49 | convolution fusion | flops 2062909440 | bytes 7133184 | tf_op jit(solution)/shard_map/bld,df->blf/dot_general | solution.py:114
  70.1 0.8 fusion.51
  70.9 1.1 fusion.97
  72.3 5.4 %fusion.36 = bf16[8,256,216]{1,2,0:T(8,128)(2,1)} fusion(bf16[8,256,1152]{1,2,0:T(8,128)(2,1)S(1)} %fusion.4, f32[8,1152]{1,0:T(8,128)S(1)} %get-tuple-element.36, f32[8,1152]{1,0:T(8,128)S(1)} %get-tuple-element.37, bf16[1152,216]{0,1:T(8,128)(2,1)S(1)} %copy-done.6), kind=kOutput, calls=%fused_computation.52 | convolution fusion | flops 1029095424 | bytes 6174720 | tf_op jit(solution)/shard_map/bld,df->blf/dot_general | solution.py:114
  77.7 3.2 fusion.98
  81.0 11.7 %fusion.39 = f32[16,256,1152]{1,2,0:T(8,128)} fusion(f32[16,256]{1,0:T(8,128)S(1)} %fusion.97, bf16[16,256,1,3,72]{1,4,3,0,2:T(8,128)(2,1)S(1)} %bitcast.197, f32[16,256,256]{1,2,0:T(8,128)} %copy-done.5, bf16[72,1152]{1,0:T(8,128)(2,1)S(1)} %copy-done.9), kind=kOutput, calls=%fused_computation.55 | convolution fusion | flops 836014336 | bytes 28035072 | tf_op jit(solution)/shard_map/blf,fd->bld/dot_general | solution.py:174
  92.7 2.1 fusion.47
  94.7 11.0 %fusion.99 = bf16[144,8,8,256]{3,1,0,2:T(8,128)(2,1)S(1)} fusion(f32[16,256,1152]{1,2,0:T(8,128)} %fusion.39, f32[8,1152]{1,0:T(8,128)S(1)} %fusion.69, f32[8,1152]{1,0:T(8,128)S(1)} %get-tuple-element.46, bf16[8,256,72]{1,2,0:T(8,128)(2,1)S(1)} %fusion.47, bf16[72,1152]{1,0:T(8,128)(2,1)S(1)} %copy-done.10, f32[8,1152]{1,0:T(8,128)S(1)} %get-tuple-element.35), kind=kOutput, calls=%fused_computation.135 | convolution fusion | flops 353894400 | bytes 24164352 | tf_op jit(solution)/shard_map/blf,fd->bld/dot_general | solution.py:177
  105.8 2.8 copy.190
  108.8 69.7 %reduce-scatter.11.cloned.1.call-done = bf16[72,2048]{1,0:T(8,128)(2,1)} async-done(((bf16[1152,2048]{1,0:T(8,128)(2,1)}), bf16[72,2048]{1,0:T(8,128)(2,1)}) %reduce-scatter.11.cloned.1.call-update) | async-done | bytes 294928
  178.5 1.0 copy.191
  179.5 0.8 copy.177
  180.4 1.0 convert_element_type.156
  181.4 35.4 %all-gather.6.cloned.1.call-done = bf16[128,256,72]{1,2,0:T(8,128)(2,1)} async-done(((bf16[8,256,72]{1,2,0:T(8,128)(2,1)}), bf16[128,256,72]{1,2,0:T(8,128)(2,1)}) %all-gather.6.cloned.1.call-update) | async-done | bytes 4718608 | tf_op jit(solution)/shard_map/all_gather | solution.py:191
  216.8 2.6 copy.153
  219.5 2.3 fusion.46
  221.8 0.9 copy-done.17
  223.1 1.5 fusion.63
  224.5 3.8 fusion.43
  228.4 3.8 fusion.40
  232.1 1.5 convert_reduce_fusion.1
  233.8 4.0 multiply_reduce_fusion.2
  238.2 6.1 %multiply_reduce_fusion = (f32[8,1152]{1,0:T(8,128)S(1)}, bf16[1152,216]{0,1:T(8,128)(2,1)S(1)}) fusion(f32[1152,216]{0,1:T(8,128)} %convert_element_type.156, f32[8,216]{1,0:T(8,128)S(1)} %mul.229, f32[8,1152]{1,0:T(8,128)S(1)} %get-tuple-element.36, f32[8,1152]{1,0:T(8,128)S(1)} %get-tuple-element.37, bf16[8,256,1152]{1,2,0:T(8,128)(2,1)} %copy-done.3, ...), kind=kOutput, calls=%fused_computation.23 | convolution fusion | flops 1030901760 | bytes 7213824 | tf_op jit(solution)/shard_map/bld,blf->bdf/dot_general | solution.py:204
  244.3 0.7 pad_maximum_fusion
  245.1 0.9 copy.180
  246.0 1.1 copy.178
  247.2 0.6 copy.162
  247.8 6.8 %all-to-all-start.1 = ((bf16[8,8,144]{2,0,1:T(8,128)(2,1)}), bf16[8,8,144]{2,0,1:T(8,128)(2,1)S(1)}, u32[]{:S(2)}, u32[]{:S(2)}) async-start(bf16[8,8,144]{2,0,1:T(8,128)(2,1)} %copy.162), calls=%async_computation.1 | async-start | bytes 65536 | tf_op jit(solution)/shard_map/all_to_all | solution.py:221
  255.9 103.5 %all-reduce.3.cloned.1.call-done = f32[8,3,1152]{2,0,1:T(8,128)} async-done(((f32[8,3,1152]{2,0,1:T(8,128)}), f32[8,3,1152]{2,0,1:T(8,128)}) %all-reduce.3.cloned.1.call-update) | async-done | bytes 110608
  359.4 0.8 constant_dynamic-slice_fusion
  360.2 34.5 %all_gather.15 = f32[64,3,72]{2,0,1:T(8,128)S(1)} all-gather(f32[8,3,72]{2,0,1:T(8,128)S(1)} %constant_dynamic-slice_fusion), channel_id=1, replica_groups=mesh['dp'=8,'tensor'=16] {'dp'}, dimensions={0}, use_global_device_ids=true | all-gather | bytes 62208 | tf_op jit(solution)/shard_map/all_gather | solution.py:220
  394.9 0.8 copy.164
  395.8 34.5 %reduce-scatter.15.cloned.1.call-done = bf16[144,72]{1,0:T(8,128)(2,1)} async-done(((bf16[1152,72]{1,0:T(8,128)(2,1)}), bf16[144,72]{1,0:T(8,128)(2,1)}) %reduce-scatter.15.cloned.1.call-update) | async-done | bytes 20752
  430.3 0.8 copy.181
  431.1 0.6 convert_element_type.155
  431.8 73.3 %reduce-scatter.13.cloned.1.call-done = bf16[144,216]{1,0:T(8,128)(2,1)} async-done(((bf16[1152,216]{1,0:T(8,128)(2,1)}), bf16[144,216]{1,0:T(8,128)(2,1)}) %reduce-scatter.13.cloned.1.call-update) | async-done | bytes 62224
  505.1 1.0 copy.179
  506.1 0.8 copy.163
  (76 shorter events, 4.9 us)
Async XLA Ops:
  7.2 1.8 copy-start
  7.2 5.1 copy-start.12
  7.2 5.1 copy-start.13
  7.2 5.3 %copy-start.7 = (bf16[3,1152,72]{1,2,0:T(8,128)(2,1)S(1)}, bf16[3,1152,72]{1,2,0:T(8,128)(2,1)}, u32[]{:S(2)}) copy-start(bf16[3,1152,72]{1,2,0:T(8,128)(2,1)} %param.24) | copy-start | bytes 1492996
  7.2 5.6 %copy-start.8 = (bf16[3,1152,72]{1,2,0:T(8,128)(2,1)S(1)}, bf16[3,1152,72]{1,2,0:T(8,128)(2,1)}, u32[]{:S(2)}) copy-start(bf16[3,1152,72]{1,2,0:T(8,128)(2,1)} %param.27) | copy-start | bytes 1492996
  7.2 12.7 %copy-start.14 = (f32[32]{0:T(128)S(1)}, f32[32]{0:T(128)}, u32[]{:S(2)}) copy-start(f32[32]{0:T(128)} %param.21) | copy-start | bytes 388
  7.2 48.5 %all-gather.4.cloned.1.call-start = ((), (), s32[]{:S(2)}) async-start(), calls=%async_computation.5 | async-start | bytes 5013504 | tf_op jit(solution)/shard_map/all_gather | solution.py:139
  14.0 20.5 %all-to-all-start = ((f32[16,24,3,72]{3,1,2,0:T(8,128)}), f32[16,24,3,72]{3,1,2,0:T(8,128)S(1)}, u32[]{:S(2)}, u32[]{:S(2)}) async-start(f32[16,24,3,72]{3,1,2,0:T(8,128)} %broadcast_in_dim.10), calls=%async_computation | async-start | bytes 1179648 | tf_op jit(solution)/shard_map/all_to_all | solution.py:19
  19.9 158.6 %reduce-scatter.11.cloned.1.call-start = ((), (), s32[]{:S(2)}) async-start(), calls=%async_computation.7 | async-start | bytes 5013504
  55.7 3.8 copy-start.2
  59.5 1.2 copy-start.11
  60.6 11.3 %copy-start.3 = (bf16[8,256,1152]{1,2,0:T(8,128)(2,1)}, bf16[8,256,1152]{1,2,0:T(8,128)(2,1)S(1)}, u32[]{:S(2)}) copy-start(bf16[8,256,1152]{1,2,0:T(8,128)(2,1)S(1)} %fusion.4) | copy-start | bytes 14155780
  70.9 6.8 %copy-start.5 = (f32[16,256,256]{1,2,0:T(8,128)}, f32[16,256,256]{1,2,0:T(8,128)S(1)}, u32[]{:S(2)}) copy-start(f32[16,256,256]{1,2,0:T(8,128)S(1)} %fusion.51) | copy-start | bytes 12582916
  70.9 1.4 copy-start.6
  72.3 8.7 %copy-start.9 = (bf16[72,1152]{1,0:T(8,128)(2,1)S(1)}, bf16[72,1152]{1,0:T(8,128)(2,1)}, u32[]{:S(2)}) copy-start(bf16[72,1152]{1,0:T(8,128)(2,1)} %param.23) | copy-start | bytes 497668
  92.7 2.1 copy-start.10
  94.7 11.0 %copy-start.16 = (bf16[8,256,72]{1,2,0:T(8,128)(2,1)}, bf16[8,256,72]{1,2,0:T(8,128)(2,1)S(1)}, u32[]{:S(2)}) copy-start(bf16[8,256,72]{1,2,0:T(8,128)(2,1)S(1)} %fusion.47) | copy-start | bytes 884740
  108.6 108.2 %all-gather.6.cloned.1.call-start = ((), (), s32[]{:S(2)}) async-start(), calls=%async_computation.6 | async-start | bytes 5013504 | tf_op jit(solution)/shard_map/all_gather | solution.py:191
  180.3 179.1 %all-reduce.3.cloned.1.call-start = ((), (), s32[]{:S(2)}) async-start(), calls=%async_computation.10 | async-start | bytes 221184
  219.5 3.6 copy-start.4
  219.5 3.2 copy-start.17
  238.2 16.4 %copy-start.15 = (u32[128]{0:T(128)S(1)}, u32[128]{0:T(128)}, u32[]{:S(2)}) copy-start(u32[128]{0:T(128)} %constant.33) | copy-start | bytes 1540
  238.2 268.6 %copy-start.1 = (bf16[1000,1152]{1,0:T(8,128)(2,1)S(1)}, bf16[1000,1152]{1,0:T(8,128)(2,1)}, u32[]{:S(2)}) copy-start(bf16[1000,1152]{1,0:T(8,128)(2,1)} %param.19) | copy-start | bytes 6912004
  245.0 185.3 %reduce-scatter.15.cloned.1.call-start = ((), (), s32[]{:S(2)}) async-start(), calls=%async_computation.9 | async-start | bytes 331776
  246.0 259.1 %reduce-scatter.13.cloned.1.call-start = ((), (), s32[]{:S(2)}) async-start(), calls=%async_computation.8 | async-start | bytes 663552
  247.8 146.8 %all-to-all-start.1 = ((bf16[8,8,144]{2,0,1:T(8,128)(2,1)}), bf16[8,8,144]{2,0,1:T(8,128)(2,1)S(1)}, u32[]{:S(2)}, u32[]{:S(2)}) async-start(bf16[8,8,144]{2,0,1:T(8,128)(2,1)} %copy.162), calls=%async_computation.1 | async-start | bytes 65536 | tf_op jit(solution)/shard_map/all_to_all | solution.py:221
Sparse Core Ops, SparseCore 0:
  9.7 45.9 all-gather.3
  108.7 69.7 reduce-scatter.10
  180.4 36.3 all-gather.5
  245.1 114.1 all-reduce.2
  362.8 67.4 reduce-scatter.14
  433.7 71.3 reduce-scatter.12
